TPU v7x, 32 devices: a whole 2x2x4 slice. The times are simulated.
32 devices in a mesh: dp: 2 (over x), expert: 4 (over z), tensor: 4 (over y, core).
Axes of the slice: x: 2, y: 2, z: 4, core: 2. Of those that a mesh axis runs over, the one named last changes fastest.
Arguments:
- tokens: bfloat16 [1024, 7168], P(('dp', 'expert'), 'tensor'), may hold values from -6 to 6
- expert_ids: int32 [1024, 2], P(('dp', 'expert')), may hold values from 0 to 3, all different within a row; in each aligned block of 128 rows (0 to 127, 128 to 255, ...) at most 96 rows name the same one
- gate_scores: bfloat16 [1024, 2], P(('dp', 'expert')), may hold values from 0.099609375 to 0.59765625
- weight_in: bfloat16 [4, 2, 7168, 1024], P('expert', None, 'tensor', 'dp'), may hold values from -0.0625 to 0.0625
- weight_out: bfloat16 [4, 1024, 7168], P('expert', 'dp', 'tensor'), may hold values from -0.1875 to 0.1875
Outputs:
- mixed: bfloat16 [1024, 7168], P(('dp', 'expert'), 'tensor')
Inputs may be any that keep to these rules, and one draw needn't show every extreme that they name: `expert_ids`: each token names 2 different experts; among the 128 tokens of one index of dp and expert together (aligned blocks of rows) no expert is named more than 96 times, and in some blocks an expert is named exactly 96 times.
All inputs are finite; a program needn't handle non-finite values.
Results may differ from a plain program's by a relative error of at most 0.0071.
Values may be sent and summed in bfloat16 or wider, within the bound.
A program may use at most 64 MiB of HBM per device.

v0:
```python
import functools

import jax
import jax.numpy as jnp
from jax import lax
from jax.experimental import pallas as pl
from jax.experimental.pallas import tpu as pltpu
from jax.sharding import PartitionSpec as P

MESH = pl.DeviceIdType.MESH
F32 = jnp.float32
BF16 = jnp.bfloat16


def dot(a, b):
    return jnp.dot(a, b, preferred_element_type=F32)


def kernel(
    sizes,
    tokens,
    ids,
    scores,
    w_in_hbm,
    w_out_hbm,
    mixed,
    w_in,
    w_out,
    squares,
    normed,
    slot_t,
    combine,
    outgoing,
    rows_in,
    part,
    part_in,
    hidden,
    keep,
    down,
    down_in,
    home,
    home_in,
    w_sem,
    sq,
    rq,
    sz,
    rz,
    sx,
    rx,
    sp,
    rp,
    sh,
    rh,
    so,
    ro,
    sr,
    rr,
):
    n_dp, n_ex, n_t, cap = sizes
    d, e, t = lax.axis_index("dp"), lax.axis_index("expert"), lax.axis_index("tensor")
    group = n_ex // n_t
    ec = e // group
    tok, width = tokens.shape
    top = ids.shape[1]
    units = w_out.shape[0]
    sub = units // n_t
    width_all = width * n_t

    def at(index, step, count):
        return lax.rem(index + step + count, count)

    def copy(src, dst, send, recv, axis, index):
        return pltpu.make_async_remote_copy(
            src_ref=src, dst_ref=dst, send_sem=send, recv_sem=recv,
            device_id={axis: index}, device_id_type=MESH,
        )

    barrier = pltpu.get_barrier_semaphore()
    for axis, me, count in (("dp", d, n_dp), ("expert", e, n_ex), ("tensor", t, n_t)):
        for step in range(1, count):
            pl.semaphore_signal(
                barrier, inc=1, device_id={axis: at(me, step, count)}, device_id_type=MESH
            )
    load_in = pltpu.make_async_copy(w_in_hbm.at[0], w_in, w_sem.at[0])
    load_out = pltpu.make_async_copy(w_out_hbm.at[0], w_out, w_sem.at[1])
    load_in.start()
    load_out.start()

    tok_rows = lax.broadcasted_iota(jnp.int32, (tok, tok), 0)
    tok_lanes = lax.broadcasted_iota(jnp.int32, (tok, tok), 1)

    def as_row(column):
        return jnp.sum(jnp.where(tok_rows == tok_lanes, column, 0.0), axis=0, keepdims=True)

    def as_column(row):
        return jnp.sum(jnp.where(tok_rows == tok_lanes, row, 0.0), axis=1, keepdims=True)

    wide = tokens[...].astype(F32)
    squares[t] = jnp.broadcast_to(as_row(jnp.sum(wide * wide, axis=1, keepdims=True)), (8, tok))

    def square_copy(step):
        return copy(squares.at[t], squares.at[t], sq.at[step], rq.at[t], "tensor", at(t, step, n_t))

    pl.semaphore_wait(barrier, n_dp + n_ex + n_t - 3)
    for step in range(1, n_t):
        square_copy(step).start()

    wide_ex = max(128, n_ex)
    ex_rows = lax.broadcasted_iota(jnp.int32, (wide_ex, tok), 0).astype(F32)
    named_t = ex_rows < 0.0
    for k in range(top):
        named_t = named_t | (ex_rows == as_row(ids[:, k : k + 1].astype(F32)))
    count_t = dot(named_t.astype(F32).astype(BF16), (tok_rows < tok_lanes).astype(F32).astype(BF16))
    slot_t[...] = jnp.where(named_t, count_t, -1.0)
    slot_rows = lax.broadcasted_iota(jnp.int32, (cap, tok), 0).astype(F32)

    for step in range(1, n_t):
        s = at(t, step, n_t)
        copy(squares.at[s], squares.at[s], sq.at[step], rq.at[s], "tensor", s).wait_recv()
    total_row = squares[0, 0:1, :]
    for s in range(1, n_t):
        total_row = total_row + squares[s, 0:1, :]
    scale = as_column(lax.rsqrt(total_row / width_all + 1e-06))
    normed[...] = (tokens[...].astype(F32) * scale).astype(BF16)

    def picked(expert):
        pick = (slot_rows == slot_t[pl.ds(expert, 1), :]).astype(F32).astype(BF16)
        return dot(pick, normed[...]).astype(BF16)

    def block(ref, lead, expert):
        if group == 1:
            return ref.at[lead, expert]
        return ref.at[lead, expert // group, pl.ds(pl.multiple_of(lax.rem(expert, group) * cap, cap), cap)]

    def send_z(expert):
        return copy(outgoing.at[expert], block(rows_in, 0, e), sz.at[expert], rz.at[e], "expert", expert)

    def wait_z(source):
        return copy(outgoing.at[source], block(rows_in, 0, source), sz.at[source], rz.at[source], "expert", source)

    def forward_x(src, expert, hop):
        return copy(
            src, block(rows_in, n_dp - hop, expert),
            sx.at[hop, expert], rx.at[n_dp - hop, expert], "dp", at(d, hop, n_dp),
        )

    def wait_x(expert, h):
        return copy(
            block(rows_in, 0, expert), block(rows_in, h, expert),
            sx.at[h, expert], rx.at[h, expert], "dp", at(d, h, n_dp),
        )

    outgoing[e] = picked(e)
    own = pltpu.make_async_copy(outgoing.at[e], block(rows_in, 0, e), w_sem.at[2])
    own.start()
    for hop in range(1, n_dp):
        forward_x(outgoing.at[e], e, hop).start()

    @pl.loop(1, n_ex)
    def _(step):
        expert = at(e, step, n_ex)
        outgoing[expert] = picked(expert)
        send_z(expert).start()

    ex_lanes = lax.broadcasted_iota(jnp.int32, (tok, wide_ex), 1)
    named = ex_lanes == ids[:, 0:1]
    for k in range(1, top):
        named = named | (ex_lanes == ids[:, k : k + 1])
    counts = dot((tok_lanes < tok_rows).astype(F32).astype(BF16), named.astype(F32).astype(BF16))
    lanes = lax.broadcasted_iota(jnp.int32, (tok, n_ex * cap), 1).astype(F32)
    weights = jnp.zeros((tok, n_ex * cap), F32)
    for k in range(top):
        this = ids[:, k : k + 1]
        slot = jnp.sum(jnp.where(ex_lanes == this, counts, 0.0), axis=1, keepdims=True)
        target = this.astype(F32) * cap + slot
        weights = weights + jnp.where(lanes == target, scores[:, k : k + 1].astype(F32), 0.0)
    combine[...] = weights.astype(BF16)

    own.wait()
    load_in.wait()
    load_out.wait()

    def part_copy(h, c, step):
        to = at(t, step, n_t)
        return copy(part.at[h, c, to], part_in.at[h, c, t], sp.at[h, c, step], rp.at[h, c, t], "tensor", to)

    def hidden_copy(h, c, step):
        to = at(t, step, n_t)
        return copy(hidden.at[h, c, t], hidden.at[h, c, t], sh.at[h, c, step], rh.at[h, c, t], "tensor", to)

    def down_copy(h, c):
        return copy(down.at[h, c], down_in.at[n_dp - h, c], so.at[h, c], ro.at[n_dp - h, c], "dp", at(d, h, n_dp))

    def project(h, c):
        @pl.when(h == 0)
        def _():
            for i in range(group):
                source = c * group + i

                @pl.when(source != e)
                def _():
                    wait_z(source).wait_recv()
                    for hop in range(1, n_dp):
                        forward_x(block(rows_in, 0, source), source, hop).start()

        @pl.when(h > 0)
        def _():
            for i in range(group):
                wait_x(c * group + i, h).wait_recv()

        rows = rows_in[h, c]
        for g in range(2):
            sums = dot(rows, w_in[g]).astype(BF16)
            for to in range(n_t):
                part[h, c, to, :, g * sub : (g + 1) * sub] = sums[:, to * sub : (to + 1) * sub]
        for step in range(1, n_t):
            part_copy(h, c, step).start()

    def activate(h, c):
        total = part[h, c, t].astype(F32)
        for step in range(1, n_t):
            s = at(t, step, n_t)
            copy(part.at[h, c, s], part_in.at[h, c, s], sp.at[h, c, step], rp.at[h, c, s], "tensor", s).wait_recv()
            total = total + part_in[h, c, s].astype(F32)
        gate, up = total[:, :sub], total[:, sub:]
        hidden[h, c, t] = (gate / (1.0 + jnp.exp(-gate)) * up).astype(BF16)
        for step in range(1, n_t):
            hidden_copy(h, c, step).start()

    def expand(h, c):
        for step in range(1, n_t):
            s = at(t, step, n_t)
            copy(hidden.at[h, c, s], hidden.at[h, c, s], sh.at[h, c, step], rh.at[h, c, s], "tensor", s).wait_recv()
        full = jnp.concatenate([hidden[h, c, s] for s in range(n_t)], axis=1)
        result = dot(full, w_out[...])

        @pl.when(h == 0)
        def _():
            keep[c] = result

        @pl.when(h > 0)
        def _():
            down[h, c] = result.astype(BF16)

            @pl.when(c != ec)
            def _():
                down_copy(h, c).start()

            @pl.when((c == at(ec, 1, n_t)) & (h == n_dp - 1))
            def _():
                for far in range(1, n_dp):
                    down_copy(far, ec).start()

    def home_copy(expert):
        return copy(block(home, 0, expert), home_in.at[e], sr.at[expert], rr.at[e], "expert", expert)

    def collect(step):
        q = at(ec, -1 - step, n_t)
        total = keep[q]
        for h in range(1, n_dp):
            copy(down.at[h, q], down_in.at[h, q], so.at[h, q], ro.at[h, q], "dp", at(d, h, n_dp)).wait_recv()
            total = total + down_in[h, q].astype(F32)
        home[0, q] = total.astype(BF16)
        for i in range(group):
            expert = q * group + i

            @pl.when(expert != e)
            def _():
                home_copy(expert).start()

            @pl.when(expert == e)
            def _():
                home_in[expert] = home[0, q, i * cap : (i + 1) * cap, :]

    def item(number):
        return lax.rem(number, n_dp), at(ec, -(number // n_dp), n_t)

    items = n_dp * n_t

    @pl.loop(0, items + 2 + 1)
    def _(step):
        @pl.when(step < items)
        def _():
            project(*item(step))

        @pl.when((step > 0) & (step <= items))
        def _():
            activate(*item(step - 1))

        @pl.when((step > 1) & (step < items + 2))
        def _():
            expand(*item(step - 2))

        for k in range(1, n_t):

            @pl.when(step == (k + 1) * n_dp + 2)
            def _():
                collect(k - 1)

    collect(n_t - 1)

    @pl.loop(1, n_ex)
    def _(step):
        source = at(e, step, n_ex)
        copy(block(home, 0, source), home_in.at[source], sr.at[source], rr.at[source], "expert", source).wait_recv()

    mixed[...] = dot(combine[...], home_in[...].reshape(n_ex * cap, width)).astype(BF16)

    @pl.loop(1, n_ex)
    def _(step):
        expert = at(e, step, n_ex)
        send_z(expert).wait_send()
        home_copy(expert).wait_send()

    @pl.loop(0, n_ex)
    def _(expert):
        for hop in range(1, n_dp):
            forward_x(block(rows_in, 0, expert), expert, hop).wait_send()

    for step in range(1, n_t):
        square_copy(step).wait_send()

    @pl.loop(0, n_t)
    def _(c):
        for h in range(n_dp):
            for step in range(1, n_t):
                part_copy(h, c, step).wait_send()
                hidden_copy(h, c, step).wait_send()
        for h in range(1, n_dp):
            down_copy(h, c).wait_send()


def per_device(sizes, tokens, expert_ids, gate_scores, weight_in, weight_out):
    n_dp, n_ex, n_t, cap = sizes
    tok, width = tokens.shape
    units = weight_out.shape[1]
    chunk = n_ex // n_t * cap
    dma = pltpu.SemaphoreType.DMA
    vmem = pl.BlockSpec(memory_space=pltpu.VMEM)
    return pl.pallas_call(
        functools.partial(kernel, sizes),
        out_shape=jax.ShapeDtypeStruct((tok, width), BF16),
        in_specs=[vmem] * 3 + [pl.BlockSpec(memory_space=pl.ANY)] * 2,
        out_specs=vmem,
        scratch_shapes=[
            pltpu.VMEM((2, width, units), BF16),
            pltpu.VMEM((units, width), BF16),
            pltpu.VMEM((n_t, 8, tok), F32),
            pltpu.VMEM((tok, width), BF16),
            pltpu.VMEM((max(128, n_ex), tok), F32),
            pltpu.VMEM((tok, n_ex * cap), BF16),
            pltpu.VMEM((n_ex, cap, width), BF16),
            pltpu.VMEM((n_dp, n_t, chunk, width), BF16),
            pltpu.VMEM((n_dp, n_t, n_t, chunk, 2 * units // n_t), BF16),
            pltpu.VMEM((n_dp, n_t, n_t, chunk, 2 * units // n_t), BF16),
            pltpu.VMEM((n_dp, n_t, n_t, chunk, units // n_t), BF16),
            pltpu.VMEM((n_t, chunk, width), F32),
            pltpu.VMEM((n_dp, n_t, chunk, width), BF16),
            pltpu.VMEM((n_dp, n_t, chunk, width), BF16),
            pltpu.VMEM((1, n_t, chunk, width), BF16),
            pltpu.VMEM((n_ex, cap, width), BF16),
            dma((3,)),
            dma((n_t,)),
            dma((n_t,)),
            dma((n_ex,)),
            dma((n_ex,)),
            dma((n_dp, n_ex)),
            dma((n_dp, n_ex)),
            dma((n_dp, n_t, n_t)),
            dma((n_dp, n_t, n_t)),
            dma((n_dp, n_t, n_t)),
            dma((n_dp, n_t, n_t)),
            dma((n_dp, n_t)),
            dma((n_dp, n_t)),
            dma((n_ex,)),
            dma((n_ex,)),
        ],
        compiler_params=pltpu.CompilerParams(
            collective_id=0, has_side_effects=True, vmem_limit_bytes=60 * 1024 * 1024
        ),
    )(tokens, expert_ids, gate_scores, weight_in, weight_out)


def solution(mesh):
    n_dp, n_ex, n_t = mesh.shape["dp"], mesh.shape["expert"], mesh.shape["tensor"]

    def whole(tokens, expert_ids, gate_scores, weight_in, weight_out):
        tok = tokens.shape[0] // (n_dp * n_ex)
        slots = min(3 * tok * expert_ids.shape[1] // (2 * n_ex), tok)
        cap = -(-slots // 16) * 16
        return jax.shard_map(
            functools.partial(per_device, (n_dp, n_ex, n_t, cap)),
            mesh=mesh,
            in_specs=(
                P(("dp", "expert"), "tensor"),
                P(("dp", "expert"), None),
                P(("dp", "expert"), None),
                P("expert", None, "tensor", "dp"),
                P("expert", "dp", "tensor"),
            ),
            out_specs=P(("dp", "expert"), "tensor"),
            check_vma=False,
        )(tokens, expert_ids, gate_scores, weight_in, weight_out)

    return whole
```

profile of v0, /device:TPU:0, one launch (start us, length us, event | category | flops | bytes accessed | tf_op | source)
XLA Modules:
  0.0 101.2 jit_solution(9996795186560438425)
XLA Ops:
  0.0 1.4 %copy.7.scores = bf16[128,2]{1,0:T(8,128)(2,1)} copy(bf16[128,2]{0,1:T(2,128)(2,1)} %param.7) | data formatting | bytes 1024 | tf_op args[2]
  1.4 1.4 %copy.6.ids = s32[128,2]{1,0:T(8,128)} copy(s32[128,2]{0,1:T(2,128)} %param.6) | data formatting | bytes 2048 | tf_op args[1]
  2.8 96.6 %shard_map.55 = bf16[128,1792]{1,0:T(8,128)(2,1)} custom-call(bf16[128,1792]{1,0:T(8,128)(2,1)} %tokens.1, s32[128,2]{1,0:T(8,128)} %copy.6.ids, bf16[128,2]{1,0:T(8,128)(2,1)} %copy.7.scores, bf16[1,2,1792,512]{3,2,1,0:T(8,128)(2,1)} %w_in_hbm.1, bf16[1,512,1792]{2,1,0:T(8,128)(2,1)} %w_out_hbm.1), custom_call_target="tpu_custom_call" | custom-call | tf_op jit(solution)/shard_map/pallas_call | solution.py:340
  99.4 1.8 %copy.9 = bf16[128,1792]{1,0:T(8,128)(2,1)} copy(bf16[128,1792]{1,0:T(8,128)(2,1)} %shard_map.55) | data formatting | bytes 917504
where the time goes:
time: 101 us
  Pallas kernels  96.6 us (96%)
  local copies, waits for them, and re-layouts  4.6 us (5%)
    pallas_call x1, Pallas kernels, per_device(): pl.pallas_call(functools.partial(kernel, sizes), out_shape=jax.ShapeDtype...  96.6 us
    unnamed x3, local copies, waits for them, and re-layouts  4.6 us

commit v1 on v0

v1 whole, which is shorter than its diff:
```python
import functools

import jax
import jax.numpy as jnp
from jax import lax
from jax.experimental import pallas as pl
from jax.experimental.pallas import tpu as pltpu
from jax.sharding import PartitionSpec as P

MESH = pl.DeviceIdType.MESH
F32 = jnp.float32
BF16 = jnp.bfloat16
SEND, FORWARD, PROJECT, ACTIVATE, EXPAND, COLLECT = range(6)
EXTRA = 16
KINDS = "SFPAEC"
TUNED = (
    "S000", "F000", "S010", "S011", "S001", "F001", "P001", "P000", "F010", "A001",
    "S030", "A000", "S031", "F011", "P100", "P101", "P010", "F030", "S020", "A100",
    "P110", "E000", "A010", "E100", "P030", "F031", "P130", "P011", "A030", "S021",
    "A101", "P031", "A110", "F020", "P111", "A031", "E110", "P131", "E010", "C000",
    "P120", "F021", "P021", "P020", "A111", "A011", "E101", "A130", "A131", "E030",
    "A120", "P121", "E130", "E131", "C010", "E001", "A020", "A121", "E011", "E031",
    "E121", "C030", "A021", "C001", "E111", "E021", "E120", "C031", "C021", "E020",
    "C011", "C020",
)


def dot(a, b):
    return jnp.dot(a, b, preferred_element_type=F32)


def lookup(values, index):
    base = 1 << max(values).bit_length()
    share = 1
    while base ** (share + 1) < 2**31:
        share += 1
    word = 0
    for i in range(0, len(values), share):
        packed = sum(v * base**k for k, v in enumerate(values[i : i + share]))
        word = jnp.where(index // share == i // share, packed, word)
    place, value = lax.rem(index, share), word
    for k in range(1, share):
        value = jnp.where(place == k, word // base**k, value)
    return lax.rem(value, base)


def make_plan(n_dp, chunks, parts):
    if (n_dp, chunks, parts) == (2, 4, 2):
        return [(KINDS.index(c[0]), *map(int, c[1:])) for c in TUNED]
    own = [(0, p) for p in range(parts)]
    offsets = sorted(range(1, chunks), key=lambda o: (o == 1, o))
    far = [(o, p) for o in offsets for p in range(parts)]
    units = own + far
    plan = []
    for o, p in own:
        plan += [(SEND, 0, o, p)]
    plan += [(SEND, 0, o, p) for o, p in far]
    for o, p in own:
        plan += [(FORWARD, 0, o, p)]
    count = len(units)
    for s in range(count + 4):
        if parts <= s + 1 < count:
            plan.append((FORWARD, 0, *units[s + 1]))
        for kind in (PROJECT, ACTIVATE, EXPAND):
            if s < count:
                plan.append((kind, 0, *units[s]))
            if 0 <= s - 1 < count:
                plan += [(kind, h, *units[s - 1]) for h in range(1, n_dp)]
        if 0 <= s - 3 < count:
            plan.append((COLLECT, 0, *units[s - 3]))
    return plan


def kernel(
    sizes,
    plan,
    tokens_hbm,
    ids,
    scores,
    w_in_hbm,
    w_out_hbm,
    mixed,
    tokens,
    w_in,
    w_out,
    slot_t,
    outgoing,
    rows_in,
    part,
    part_in,
    hidden,
    keep,
    down,
    down_in,
    home,
    home_in,
    local_sem,
    sz,
    rz,
    sx,
    rx,
    sp,
    rp,
    sh,
    rh,
    so,
    ro,
    sr,
    rr,
):
    n_dp, n_ex, n_t, cap, group, parts = sizes
    d, e, t = lax.axis_index("dp"), lax.axis_index("expert"), lax.axis_index("tensor")
    chunks = n_ex // group
    piece = cap // parts
    ec, ei = e // group, lax.rem(e, group)
    tok, width = tokens.shape
    top = ids.shape[0]
    units = w_out.shape[0]
    sub = units // n_t
    rows = group * piece
    width_all = width * n_t

    def at(index, step, count):
        return lax.rem(index + step + count, count)

    def copy(src, dst, send, recv, axis, index):
        return pltpu.make_async_remote_copy(
            src_ref=src, dst_ref=dst, send_sem=send, recv_sem=recv,
            device_id={axis: index}, device_id_type=MESH,
        )

    load_tokens = pltpu.make_async_copy(tokens_hbm, tokens, local_sem.at[0])
    load_in = pltpu.make_async_copy(w_in_hbm.at[0], w_in, local_sem.at[1])
    load_out = pltpu.make_async_copy(w_out_hbm.at[0], w_out, local_sem.at[2])
    load_tokens.start()
    barrier = pltpu.get_barrier_semaphore()
    for axis, me, count in (("dp", d, n_dp), ("expert", e, n_ex), ("tensor", t, n_t)):
        for step in range(1, count):
            pl.semaphore_signal(
                barrier, inc=1, device_id={axis: at(me, step, count)}, device_id_type=MESH
            )
    load_in.start()
    load_out.start()

    tok_rows = lax.broadcasted_iota(jnp.int32, (tok, tok), 0)
    tok_lanes = lax.broadcasted_iota(jnp.int32, (tok, tok), 1)
    wide_ex = max(128, n_ex)
    ex_rows = lax.broadcasted_iota(jnp.int32, (wide_ex, tok), 0)
    named_t = ex_rows < 0
    for k in range(top):
        named_t = named_t | (ex_rows == ids[k : k + 1, :])
    count_t = dot(named_t.astype(F32).astype(BF16), (tok_rows < tok_lanes).astype(F32).astype(BF16))
    slot_t[...] = jnp.where(named_t, count_t, -1.0)

    load_tokens.wait()
    pl.semaphore_wait(barrier, n_dp + n_ex + n_t - 3)

    def block(ref, lead, member, p):
        u = (member // group) * parts + p
        if group == 1:
            return ref.at[(*lead, u)]
        return ref.at[(*lead, u, pl.ds(pl.multiple_of(lax.rem(member, group) * piece, piece), piece))]

    def z_copy(expert, p):
        return copy(
            outgoing.at[expert * parts + p], block(rows_in, (0,), e, p),
            sz.at[expert * parts + p], rz.at[e * parts + p], "expert", expert,
        )

    def z_wait(source, p):
        copy(
            outgoing.at[source * parts + p], block(rows_in, (0,), source, p),
            sz.at[source * parts + p], rz.at[source * parts + p], "expert", source,
        ).wait_recv()

    def x_copy(u, hop):
        return copy(
            rows_in.at[0, u], rows_in.at[n_dp - hop, u],
            sx.at[hop, u], rx.at[n_dp - hop, u], "dp", at(d, hop, n_dp),
        )

    def part_copy(h, u, step):
        to = at(t, step, n_t)
        return copy(part.at[h, u, to], part_in.at[h, u, t], sp.at[h, u, step], rp.at[h, u, t], "tensor", to)

    def hidden_copy(h, u, step):
        to = at(t, step, n_t)
        return copy(hidden.at[h, u, t], hidden.at[h, u, t], sh.at[h, u, step], rh.at[h, u, t], "tensor", to)

    def down_copy(h, u):
        return copy(
            down.at[h - 1, u], down_in.at[n_dp - h - 1, u], so.at[h, u], ro.at[n_dp - h, u], "dp", at(d, h, n_dp)
        )

    def home_copy(expert, p):
        return copy(
            block(home, (), expert, p), home_in.at[e * parts + p],
            sr.at[expert * parts + p], rr.at[e * parts + p], "expert", expert,
        )

    def home_wait(source, p):
        copy(
            block(home, (), source, p), home_in.at[source * parts + p],
            sr.at[source * parts + p], rr.at[source * parts + p], "expert", source,
        ).wait_recv()

    piece_rows = lax.broadcasted_iota(jnp.int32, (piece, tok), 0)

    def picked(expert, p):
        want = (piece_rows + p * piece).astype(F32)
        return (want == slot_t[pl.ds(expert, 1), :]).astype(F32)

    def send(q, p):
        for i in range(group):
            expert = q * group + i
            out = dot(picked(expert, p).astype(BF16), tokens[...]).astype(BF16)

            @pl.when(expert != e)
            def _():
                outgoing[expert * parts + p] = out
                z_copy(expert, p).start()

            @pl.when(expert == e)
            def _():
                block(rows_in, (0,), e, p)[...] = out

    def forward(q, p):
        for i in range(group):
            source = q * group + i

            @pl.when(source != e)
            def _():
                z_wait(source, p)

        for hop in range(1, n_dp):
            x_copy(q * parts + p, hop).start()

    diagonal = lax.broadcasted_iota(jnp.int32, (rows, 2 * sub), 0) == lax.broadcasted_iota(jnp.int32, (rows, 2 * sub), 1)
    extra_rows = lax.broadcasted_iota(jnp.int32, (EXTRA, 2 * sub), 0)

    def project(h, u):
        @pl.when(h > 0)
        def _():
            copy(rows_in.at[0, u], rows_in.at[h, u], sx.at[h, u], rx.at[h, u], "dp", at(d, h, n_dp)).wait_recv()

        block_rows = rows_in[h, u]
        wide = block_rows.astype(F32)
        squares = jnp.sum(wide * wide, axis=1, keepdims=True)
        squares = jnp.sum(jnp.where(diagonal, squares, 0.0), axis=0, keepdims=True)
        high = squares.astype(BF16).astype(F32)
        extra = jnp.where(extra_rows == 0, high, jnp.where(extra_rows == 1, squares - high, 0.0)).astype(BF16)
        for to in range(n_t):
            part[h, u, to, rows:, :] = extra
        for g in range(2):
            sums = dot(block_rows, w_in[g]).astype(BF16)
            for to in range(n_t):
                part[h, u, to, :rows, g * sub : (g + 1) * sub] = sums[:, to * sub : (to + 1) * sub]
        for step in range(1, n_t):
            part_copy(h, u, step).start()

    def activate(h, u):
        total = part[h, u, t].astype(F32)
        for step in range(1, n_t):
            s = at(t, step, n_t)
            copy(part.at[h, u, s], part_in.at[h, u, s], sp.at[h, u, step], rp.at[h, u, s], "tensor", s).wait_recv()
            total = total + part_in[h, u, s].astype(F32)
        squares = jnp.sum(total[rows:], axis=0, keepdims=True)
        squares = jnp.sum(jnp.where(diagonal, squares, 0.0), axis=1, keepdims=True)
        total = total[:rows] * lax.rsqrt(squares / width_all + 1e-06)
        gate, up = total[:, :sub], total[:, sub:]
        hidden[h, u, t] = (gate / (1.0 + jnp.exp(-gate)) * up).astype(BF16)
        for step in range(1, n_t):
            hidden_copy(h, u, step).start()

    def expand(h, u):
        for step in range(1, n_t):
            s = at(t, step, n_t)
            copy(hidden.at[h, u, s], hidden.at[h, u, s], sh.at[h, u, step], rh.at[h, u, s], "tensor", s).wait_recv()
        full = jnp.concatenate([hidden[h, u, s] for s in range(n_t)], axis=1)
        result = dot(full, w_out[...])

        @pl.when(h == 0)
        def _():
            keep[u] = result

        @pl.when(h > 0)
        def _():
            down[h - 1, u] = result.astype(BF16)
            down_copy(h, u).start()

    def collect(q, p):
        u = q * parts + p
        total = keep[u]
        for h in range(1, n_dp):
            copy(
                down.at[h - 1, u], down_in.at[h - 1, u], so.at[h, u], ro.at[h, u], "dp", at(d, h, n_dp)
            ).wait_recv()
            total = total + down_in[h - 1, u].astype(F32)
        home[u] = total.astype(BF16)
        for i in range(group):
            expert = q * group + i

            @pl.when(expert != e)
            def _():
                home_copy(expert, p).start()

            @pl.when(expert == e)
            def _():
                home_in[expert * parts + p] = home[u, i * piece : (i + 1) * piece]

    first_project = min(i for i, op in enumerate(plan) if op[0] == PROJECT)
    first_expand = min(i for i, op in enumerate(plan) if op[0] == EXPAND)

    codes = [kind + 8 * (h + n_dp * (p + parts * o)) for kind, h, o, p in plan]

    @pl.loop(0, len(plan))
    def _(step):
        code = lookup(codes, step)
        kind, rest = lax.rem(code, 8), code // 8
        h, rest = lax.rem(rest, n_dp), rest // n_dp
        p, o = lax.rem(rest, parts), rest // parts
        to, q = lax.rem(ec + o, chunks), lax.rem(ec - o + chunks, chunks)
        u = q * parts + p

        @pl.when(kind == SEND)
        def _():
            with SCOPE("send"):
                send(to, p)

        @pl.when(kind == FORWARD)
        def _():
            with SCOPE("forward"):
                forward(q, p)

        @pl.when(kind == PROJECT)
        def _():
            @pl.when(step == first_project)
            def _():
                load_in.wait()

            with SCOPE("project"):
                project(h, u)

        @pl.when(kind == ACTIVATE)
        def _():
            with SCOPE("activate"):
                activate(h, u)

        @pl.when(kind == EXPAND)
        def _():
            @pl.when(step == first_expand)
            def _():
                load_out.wait()

            with SCOPE("expand"):
                expand(h, u)

        @pl.when(kind == COLLECT)
        def _():
            with SCOPE("collect"):
                collect(q, p)

    weights = []
    for expert in range(n_ex):
        score = jnp.zeros((1, tok), F32)
        for k in range(top):
            score = score + jnp.where(ids[k : k + 1, :] == expert, scores[k : k + 1, :].astype(F32), 0.0)
        weights += [picked(expert, p) * score for p in range(parts)]
    combine = jnp.transpose(jnp.concatenate(weights, axis=0)).astype(BF16)

    with SCOPE("homes"):
        @pl.loop(1, n_ex)
        def _(step):
            source = at(e, step, n_ex)
            for p in range(parts):
                home_wait(source, p)

    with SCOPE("mix"):
        mixed[...] = dot(combine, home_in[...].reshape(n_ex * cap, width)).astype(BF16)

    with SCOPE("drain"):
        @pl.loop(1, n_ex)
        def _(step):
            expert = at(e, step, n_ex)
            for p in range(parts):
                z_copy(expert, p).wait_send()
                home_copy(expert, p).wait_send()

        @pl.loop(0, chunks * parts)
        def _(u):
            for hop in range(1, n_dp):
                x_copy(u, hop).wait_send()
                down_copy(hop, u).wait_send()
            for h in range(n_dp):
                for step in range(1, n_t):
                    part_copy(h, u, step).wait_send()
                    hidden_copy(h, u, step).wait_send()


SCOPE = jax.named_scope


def per_device(sizes, tokens, ids, scores, weight_in, weight_out):
    n_dp, n_ex, n_t, cap, group, parts = sizes
    tok, width = tokens.shape
    units = weight_out.shape[1]
    chunks = n_ex // group
    count = chunks * parts
    piece = cap // parts
    rows = group * piece
    plan = make_plan(n_dp, chunks, parts)
    dma = pltpu.SemaphoreType.DMA
    vmem = pl.BlockSpec(memory_space=pltpu.VMEM)
    hbm = pl.BlockSpec(memory_space=pl.ANY)
    return pl.pallas_call(
        functools.partial(kernel, sizes, plan),
        out_shape=jax.ShapeDtypeStruct((tok, width), BF16),
        in_specs=[hbm, vmem, vmem, hbm, hbm],
        out_specs=vmem,
        scratch_shapes=[
            pltpu.VMEM((tok, width), BF16),
            pltpu.VMEM((2, width, units), BF16),
            pltpu.VMEM((units, width), BF16),
            pltpu.VMEM((max(128, n_ex), tok), F32),
            pltpu.VMEM((n_ex * parts, piece, width), BF16),
            pltpu.VMEM((n_dp, count, rows, width), BF16),
            pltpu.VMEM((n_dp, count, n_t, rows + EXTRA, 2 * units // n_t), BF16),
            pltpu.VMEM((n_dp, count, n_t, rows + EXTRA, 2 * units // n_t), BF16),
            pltpu.VMEM((n_dp, count, n_t, rows, units // n_t), BF16),
            pltpu.VMEM((count, rows, width), F32),
            pltpu.VMEM((n_dp - 1, count, rows, width), BF16),
            pltpu.VMEM((n_dp - 1, count, rows, width), BF16),
            pltpu.VMEM((count, rows, width), BF16),
            pltpu.VMEM((n_ex * parts, piece, width), BF16),
            dma((3,)),
            dma((n_ex * parts,)),
            dma((n_ex * parts,)),
            dma((n_dp, count)),
            dma((n_dp, count)),
            dma((n_dp, count, n_t)),
            dma((n_dp, count, n_t)),
            dma((n_dp, count, n_t)),
            dma((n_dp, count, n_t)),
            dma((n_dp, count)),
            dma((n_dp, count)),
            dma((n_ex * parts,)),
            dma((n_ex * parts,)),
        ],
        compiler_params=pltpu.CompilerParams(
            collective_id=0, has_side_effects=True, vmem_limit_bytes=60 * 1024 * 1024
        ),
    )(tokens, ids, scores, weight_in, weight_out)


def solution(mesh):
    n_dp, n_ex, n_t = mesh.shape["dp"], mesh.shape["expert"], mesh.shape["tensor"]

    def whole(tokens, expert_ids, gate_scores, weight_in, weight_out):
        tok = tokens.shape[0] // (n_dp * n_ex)
        slots = min(3 * tok * expert_ids.shape[1] // (2 * n_ex), tok)
        group = max(1, n_ex // n_t)
        parts = 2 if group == 1 else 1
        cap = -(-slots // (16 * parts)) * 16 * parts
        return jax.shard_map(
            functools.partial(per_device, (n_dp, n_ex, n_t, cap, group, parts)),
            mesh=mesh,
            in_specs=(
                P(("dp", "expert"), "tensor"),
                P(None, ("dp", "expert")),
                P(None, ("dp", "expert")),
                P("expert", None, "tensor", "dp"),
                P("expert", "dp", "tensor"),
            ),
            out_specs=P(("dp", "expert"), "tensor"),
            check_vma=False,
        )(tokens, expert_ids.T, gate_scores.T, weight_in, weight_out)

    return whole
```

time: 101 us -> 89.6 us (0.89)
  Pallas kernels: 96.6 us -> 87.6 us
  local copies, waits for them, and re-layouts: 4.6 us -> 1.82 us
    pallas_call x1, Pallas kernels: 96.6 us -> 87.6 us  [per_device(): pl.pallas_call(functools.partial(kernel, sizes, plan), out_shape=jax.Shap...]
    unnamed x3 -> x1, local copies, waits for them, and re-layouts: 4.6 us -> 1.82 us
where the time goes in v1:
time: 89.6 us; the launch traced here: 89.5 us
  Pallas kernels  87.6 us (98%)
  local copies, waits for them, and re-layouts  1.82 us (2%)
    pallas_call x1, Pallas kernels, per_device(): pl.pallas_call(functools.partial(kernel, sizes, plan), out_shape=jax.Shap...  87.6 us
    unnamed x1, local copies, waits for them, and re-layouts  1.82 us

profile of v1, /device:TPU:0, one launch (start us, length us, event | category | flops | bytes accessed | tf_op | source)
XLA Modules:
  0.0 89.5 jit_solution(2544885923799905927)
XLA Ops:
  0.0 87.6 %shard_map.55 = bf16[128,1792]{1,0:T(8,128)(2,1)} custom-call(bf16[128,1792]{1,0:T(8,128)(2,1)} %tokens_hbm.1, s32[2,128]{1,0:T(2,128)} %bitcast.2, bf16[2,128]{1,0:T(2,128)(2,1)} %bitcast.3, bf16[1,2,1792,512]{3,2,1,0:T(8,128)(2,1)} %w_in_hbm.1, bf16[1,512,1792]{2,1,0:T(8,128)(2,1)} %w_out_hbm.1), custom_call_target="tpu_custom_call" | custom-call | tf_op jit(solution)/shard_map/pallas_call | solution.py:415
  87.6 1.8 %copy.7 = bf16[128,1792]{1,0:T(8,128)(2,1)} copy(bf16[128,1792]{1,0:T(8,128)(2,1)} %shard_map.55) | data formatting | bytes 917504

commit v2 on v1

--- a/solution.py
+++ b/solution.py
@@ -129,6 +129,9 @@
             device_id={axis: index}, device_id_type=MESH,
         )
 
+    def pending(like, sem):
+        return pltpu.make_async_copy(like, like, sem)
+
     load_tokens = pltpu.make_async_copy(tokens_hbm, tokens, local_sem.at[0])
     load_in = pltpu.make_async_copy(w_in_hbm.at[0], w_in, local_sem.at[1])
     load_out = pltpu.make_async_copy(w_out_hbm.at[0], w_out, local_sem.at[2])
@@ -164,45 +167,39 @@
     def z_copy(expert, p):
         return copy(
             outgoing.at[expert * parts + p], block(rows_in, (0,), e, p),
-            sz.at[expert * parts + p], rz.at[e * parts + p], "expert", expert,
+            sz, rz.at[e * parts + p], "expert", expert,
         )
 
     def z_wait(source, p):
         copy(
             outgoing.at[source * parts + p], block(rows_in, (0,), source, p),
-            sz.at[source * parts + p], rz.at[source * parts + p], "expert", source,
+            sz, rz.at[source * parts + p], "expert", source,
         ).wait_recv()
 
     def x_copy(u, hop):
         return copy(
             rows_in.at[0, u], rows_in.at[n_dp - hop, u],
-            sx.at[hop, u], rx.at[n_dp - hop, u], "dp", at(d, hop, n_dp),
+            sx, rx.at[n_dp - hop - 1, u], "dp", at(d, hop, n_dp),
         )
 
     def part_copy(h, u, step):
         to = at(t, step, n_t)
-        return copy(part.at[h, u, to], part_in.at[h, u, t], sp.at[h, u, step], rp.at[h, u, t], "tensor", to)
+        return copy(part.at[h, u, to], part_in.at[h, u, t], sp, rp.at[h, u], "tensor", to)
 
     def hidden_copy(h, u, step):
         to = at(t, step, n_t)
-        return copy(hidden.at[h, u, t], hidden.at[h, u, t], sh.at[h, u, step], rh.at[h, u, t], "tensor", to)
+        return copy(hidden.at[h, u, t], hidden.at[h, u, t], sh, rh.at[h, u], "tensor", to)
 
     def down_copy(h, u):
         return copy(
-            down.at[h - 1, u], down_in.at[n_dp - h - 1, u], so.at[h, u], ro.at[n_dp - h, u], "dp", at(d, h, n_dp)
+            down.at[h - 1, u], down_in.at[n_dp - h - 1, u], so, ro.at[n_dp - h - 1, u], "dp", at(d, h, n_dp)
         )
 
     def home_copy(expert, p):
         return copy(
             block(home, (), expert, p), home_in.at[e * parts + p],
-            sr.at[expert * parts + p], rr.at[e * parts + p], "expert", expert,
+            sr, rr, "expert", expert,
         )
-
-    def home_wait(source, p):
-        copy(
-            block(home, (), source, p), home_in.at[source * parts + p],
-            sr.at[source * parts + p], rr.at[source * parts + p], "expert", source,
-        ).wait_recv()
 
     piece_rows = lax.broadcasted_iota(jnp.int32, (piece, tok), 0)
 
@@ -241,7 +238,7 @@
     def project(h, u):
         @pl.when(h > 0)
         def _():
-            copy(rows_in.at[0, u], rows_in.at[h, u], sx.at[h, u], rx.at[h, u], "dp", at(d, h, n_dp)).wait_recv()
+            copy(rows_in.at[0, u], rows_in.at[h, u], sx, rx.at[h - 1, u], "dp", at(d, h, n_dp)).wait_recv()
 
         block_rows = rows_in[h, u]
         wide = block_rows.astype(F32)
@@ -259,11 +256,10 @@
             part_copy(h, u, step).start()
 
     def activate(h, u):
+        pending(part_in.at[h, u, : n_t - 1], rp.at[h, u]).wait()
         total = part[h, u, t].astype(F32)
         for step in range(1, n_t):
-            s = at(t, step, n_t)
-            copy(part.at[h, u, s], part_in.at[h, u, s], sp.at[h, u, step], rp.at[h, u, s], "tensor", s).wait_recv()
-            total = total + part_in[h, u, s].astype(F32)
+            total = total + part_in[h, u, at(t, step, n_t)].astype(F32)
         squares = jnp.sum(total[rows:], axis=0, keepdims=True)
         squares = jnp.sum(jnp.where(diagonal, squares, 0.0), axis=1, keepdims=True)
         total = total[:rows] * lax.rsqrt(squares / width_all + 1e-06)
@@ -273,9 +269,7 @@
             hidden_copy(h, u, step).start()
 
     def expand(h, u):
-        for step in range(1, n_t):
-            s = at(t, step, n_t)
-            copy(hidden.at[h, u, s], hidden.at[h, u, s], sh.at[h, u, step], rh.at[h, u, s], "tensor", s).wait_recv()
+        pending(hidden.at[h, u, : n_t - 1], rh.at[h, u]).wait()
         full = jnp.concatenate([hidden[h, u, s] for s in range(n_t)], axis=1)
         result = dot(full, w_out[...])
 
@@ -293,7 +287,7 @@
         total = keep[u]
         for h in range(1, n_dp):
             copy(
-                down.at[h - 1, u], down_in.at[h - 1, u], so.at[h, u], ro.at[h, u], "dp", at(d, h, n_dp)
+                down.at[h - 1, u], down_in.at[h - 1, u], so, ro.at[h - 1, u], "dp", at(d, h, n_dp)
             ).wait_recv()
             total = total + down_in[h - 1, u].astype(F32)
         home[u] = total.astype(BF16)
@@ -368,33 +362,20 @@
         weights += [picked(expert, p) * score for p in range(parts)]
     combine = jnp.transpose(jnp.concatenate(weights, axis=0)).astype(BF16)
 
+    others = (n_ex - 1) * parts
     with SCOPE("homes"):
-        @pl.loop(1, n_ex)
-        def _(step):
-            source = at(e, step, n_ex)
-            for p in range(parts):
-                home_wait(source, p)
+        pending(home_in.at[:others], rr).wait()
 
     with SCOPE("mix"):
         mixed[...] = dot(combine, home_in[...].reshape(n_ex * cap, width)).astype(BF16)
 
     with SCOPE("drain"):
-        @pl.loop(1, n_ex)
-        def _(step):
-            expert = at(e, step, n_ex)
-            for p in range(parts):
-                z_copy(expert, p).wait_send()
-                home_copy(expert, p).wait_send()
-
-        @pl.loop(0, chunks * parts)
-        def _(u):
-            for hop in range(1, n_dp):
-                x_copy(u, hop).wait_send()
-                down_copy(hop, u).wait_send()
-            for h in range(n_dp):
-                for step in range(1, n_t):
-                    part_copy(h, u, step).wait_send()
-                    hidden_copy(h, u, step).wait_send()
+        pending(outgoing.at[:others], sz).wait()
+        pending(home_in.at[:others], sr).wait()
+        pending(down, so).wait()
+        pending(rows_in.at[1:], sx).wait()
+        pending(part.at[:, :, : n_t - 1], sp).wait()
+        pending(hidden.at[:, :, : n_t - 1], sh).wait()
 
 
 SCOPE = jax.named_scope
@@ -433,18 +414,18 @@
             pltpu.VMEM((count, rows, width), BF16),
             pltpu.VMEM((n_ex * parts, piece, width), BF16),
             dma((3,)),
+            dma,
             dma((n_ex * parts,)),
-            dma((n_ex * parts,)),
+            dma,
+            dma((n_dp - 1, count)),
+            dma,
             dma((n_dp, count)),
+            dma,
             dma((n_dp, count)),
-            dma((n_dp, count, n_t)),
-            dma((n_dp, count, n_t)),
-            dma((n_dp, count, n_t)),
-            dma((n_dp, count, n_t)),
-            dma((n_dp, count)),
-            dma((n_dp, count)),
-            dma((n_ex * parts,)),
-            dma((n_ex * parts,)),
+            dma,
+            dma((n_dp - 1, count)),
+            dma,
+            dma,
         ],
         compiler_params=pltpu.CompilerParams(
             collective_id=0, has_side_effects=True, vmem_limit_bytes=60 * 1024 * 1024

time: 89.6 us -> 86.8 us (0.969)
  Pallas kernels: 87.6 us -> 84.8 us
    pallas_call x1, Pallas kernels: 87.6 us -> 84.8 us  [per_device(): pl.pallas_call(functools.partial(kernel, sizes, plan), out_shape=jax.Shap...]
where the time goes in v2:
time: 86.8 us; the launch traced here: 86.6 us
  Pallas kernels  84.8 us (98%)
  local copies, waits for them, and re-layouts  1.82 us (2%)
    pallas_call x1, Pallas kernels, per_device(): pl.pallas_call(functools.partial(kernel, sizes, plan), out_shape=jax.Shap...  84.8 us
    unnamed x1, local copies, waits for them, and re-layouts  1.82 us

profile of v2, /device:TPU:0, one launch (start us, length us, event | category | flops | bytes accessed | tf_op | source)
XLA Modules:
  0.0 86.6 jit_solution(467864070315982699)
XLA Ops:
  0.0 84.8 %shard_map.55 = bf16[128,1792]{1,0:T(8,128)(2,1)} custom-call(bf16[128,1792]{1,0:T(8,128)(2,1)} %tokens_hbm.1, s32[2,128]{1,0:T(2,128)} %bitcast.2, bf16[2,128]{1,0:T(2,128)(2,1)} %bitcast.3, bf16[1,2,1792,512]{3,2,1,0:T(8,128)(2,1)} %w_in_hbm.1, bf16[1,512,1792]{2,1,0:T(8,128)(2,1)} %w_out_hbm.1), custom_call_target="tpu_custom_call" | custom-call | tf_op jit(solution)/shard_map/pallas_call | solution.py:396
  84.8 1.8 %copy.7 = bf16[128,1792]{1,0:T(8,128)(2,1)} copy(bf16[128,1792]{1,0:T(8,128)(2,1)} %shard_map.55) | data formatting | bytes 917504

commit v3 on v2

--- a/solution.py
+++ b/solution.py
@@ -11,17 +11,17 @@
 F32 = jnp.float32
 BF16 = jnp.bfloat16
 SEND, FORWARD, PROJECT, ACTIVATE, EXPAND, COLLECT = range(6)
-EXTRA = 16
 KINDS = "SFPAEC"
 TUNED = (
-    "S000", "F000", "S010", "S011", "S001", "F001", "P001", "P000", "F010", "A001",
-    "S030", "A000", "S031", "F011", "P100", "P101", "P010", "F030", "S020", "A100",
-    "P110", "E000", "A010", "E100", "P030", "F031", "P130", "P011", "A030", "S021",
-    "A101", "P031", "A110", "F020", "P111", "A031", "E110", "P131", "E010", "C000",
-    "P120", "F021", "P021", "P020", "A111", "A011", "E101", "A130", "A131", "E030",
-    "A120", "P121", "E130", "E131", "C010", "E001", "A020", "A121", "E011", "E031",
-    "E121", "C030", "A021", "C001", "E111", "E021", "E120", "C031", "C021", "E020",
-    "C011", "C020",
+    "S011", "F001", "P001", "S012", "F002", "P000", "P002", "S031", "F011", "S030", "S032", "P011",
+    "F012", "P102", "F031", "S020", "P012", "P031", "P101", "S022", "F000", "P112", "F030", "P111",
+    "P131", "A012", "F032", "A111", "A131", "F020", "A112", "S021", "P100", "P020", "S010", "F022",
+    "A031", "P132", "A011", "A002", "E112", "E111", "P120", "P032", "P122", "P022", "E012", "E131",
+    "C012", "A020", "A120", "A132", "A032", "F021", "E011", "A122", "C011", "E031", "P021", "A022",
+    "A001", "E020", "C031", "E122", "E032", "F010", "E120", "P121", "E022", "P130", "C022", "P010",
+    "A021", "E132", "A121", "P110", "A130", "P030", "C020", "E121", "A110", "A010", "E001", "A100",
+    "E130", "A030", "C032", "A101", "A000", "E021", "C021", "E110", "E010", "A102", "E030", "E101",
+    "E100", "C030", "E102", "C010", "E002", "E000", "C000", "C001", "C002",
 )
 
 
@@ -45,15 +45,13 @@
 
 
 def make_plan(n_dp, chunks, parts):
-    if (n_dp, chunks, parts) == (2, 4, 2):
+    if (n_dp, chunks, parts) == (2, 4, 3):
         return [(KINDS.index(c[0]), *map(int, c[1:])) for c in TUNED]
     own = [(0, p) for p in range(parts)]
     offsets = sorted(range(1, chunks), key=lambda o: (o == 1, o))
     far = [(o, p) for o in offsets for p in range(parts)]
     units = own + far
     plan = []
-    for o, p in own:
-        plan += [(SEND, 0, o, p)]
     plan += [(SEND, 0, o, p) for o, p in far]
     for o, p in own:
         plan += [(FORWARD, 0, o, p)]
@@ -75,15 +73,20 @@
     sizes,
     plan,
     tokens_hbm,
-    ids,
-    scores,
+    ids_hbm,
+    scores_hbm,
     w_in_hbm,
     w_out_hbm,
     mixed,
     tokens,
+    ids,
+    scores,
     w_in,
     w_out,
     slot_t,
+    squares,
+    scale_out,
+    scales_in,
     outgoing,
     rows_in,
     part,
@@ -94,7 +97,13 @@
     down_in,
     home,
     home_in,
+    result,
     local_sem,
+    sq,
+    rq,
+    sn,
+    sm,
+    rn,
     sz,
     rz,
     sx,
@@ -123,10 +132,10 @@
     def at(index, step, count):
         return lax.rem(index + step + count, count)
 
-    def copy(src, dst, send, recv, axis, index):
+    def copy(src, dst, send, recv, **index):
         return pltpu.make_async_remote_copy(
             src_ref=src, dst_ref=dst, send_sem=send, recv_sem=recv,
-            device_id={axis: index}, device_id_type=MESH,
+            device_id=index, device_id_type=MESH,
         )
 
     def pending(like, sem):
@@ -135,13 +144,17 @@
     load_tokens = pltpu.make_async_copy(tokens_hbm, tokens, local_sem.at[0])
     load_in = pltpu.make_async_copy(w_in_hbm.at[0], w_in, local_sem.at[1])
     load_out = pltpu.make_async_copy(w_out_hbm.at[0], w_out, local_sem.at[2])
+    load_ids = pltpu.make_async_copy(ids_hbm, ids, local_sem.at[3])
+    load_scores = pltpu.make_async_copy(scores_hbm, scores, local_sem.at[4])
+    load_ids.start()
     load_tokens.start()
     barrier = pltpu.get_barrier_semaphore()
-    for axis, me, count in (("dp", d, n_dp), ("expert", e, n_ex), ("tensor", t, n_t)):
+    for axis, me, count in (("expert", e, n_ex), ("dp", d, n_dp), ("tensor", t, n_t)):
         for step in range(1, count):
             pl.semaphore_signal(
                 barrier, inc=1, device_id={axis: at(me, step, count)}, device_id_type=MESH
             )
+    load_scores.start()
     load_in.start()
     load_out.start()
 
@@ -150,13 +163,11 @@
     wide_ex = max(128, n_ex)
     ex_rows = lax.broadcasted_iota(jnp.int32, (wide_ex, tok), 0)
     named_t = ex_rows < 0
+    load_ids.wait()
     for k in range(top):
         named_t = named_t | (ex_rows == ids[k : k + 1, :])
     count_t = dot(named_t.astype(F32).astype(BF16), (tok_rows < tok_lanes).astype(F32).astype(BF16))
     slot_t[...] = jnp.where(named_t, count_t, -1.0)
-
-    load_tokens.wait()
-    pl.semaphore_wait(barrier, n_dp + n_ex + n_t - 3)
 
     def block(ref, lead, member, p):
         u = (member // group) * parts + p
@@ -167,59 +178,96 @@
     def z_copy(expert, p):
         return copy(
             outgoing.at[expert * parts + p], block(rows_in, (0,), e, p),
-            sz, rz.at[e * parts + p], "expert", expert,
+            sz, rz.at[e * parts + p], expert=expert,
         )
 
     def z_wait(source, p):
         copy(
             outgoing.at[source * parts + p], block(rows_in, (0,), source, p),
-            sz, rz.at[source * parts + p], "expert", source,
+            sz, rz.at[source * parts + p], expert=source,
         ).wait_recv()
 
     def x_copy(u, hop):
         return copy(
             rows_in.at[0, u], rows_in.at[n_dp - hop, u],
-            sx, rx.at[n_dp - hop - 1, u], "dp", at(d, hop, n_dp),
+            sx, rx.at[n_dp - hop - 1, u], dp=at(d, hop, n_dp),
         )
 
     def part_copy(h, u, step):
         to = at(t, step, n_t)
-        return copy(part.at[h, u, to], part_in.at[h, u, t], sp, rp.at[h, u], "tensor", to)
+        return copy(part.at[h, u, to], part_in.at[h, u, t], sp, rp.at[h, u], tensor=to)
 
     def hidden_copy(h, u, step):
         to = at(t, step, n_t)
-        return copy(hidden.at[h, u, t], hidden.at[h, u, t], sh, rh.at[h, u], "tensor", to)
+        return copy(hidden.at[h, u, t], hidden.at[h, u, t], sh, rh.at[h, u], tensor=to)
 
     def down_copy(h, u):
         return copy(
-            down.at[h - 1, u], down_in.at[n_dp - h - 1, u], so, ro.at[n_dp - h - 1, u], "dp", at(d, h, n_dp)
+            down.at[h - 1, u], down_in.at[n_dp - h - 1, u], so, ro.at[n_dp - h - 1, u], dp=at(d, h, n_dp)
         )
 
     def home_copy(expert, p):
         return copy(
             block(home, (), expert, p), home_in.at[e * parts + p],
-            sr, rr, "expert", expert,
+            sr, rr, expert=expert,
         )
 
     piece_rows = lax.broadcasted_iota(jnp.int32, (piece, tok), 0)
+    diagonal = piece_rows == lax.broadcasted_iota(jnp.int32, (piece, tok), 1)
 
     def picked(expert, p):
         want = (piece_rows + p * piece).astype(F32)
-        return (want == slot_t[pl.ds(expert, 1), :]).astype(F32)
+        return want == slot_t[expert : expert + 1, :]
+
+    with SCOPE("tok"):
+        load_tokens.wait()
+    for expert in range(n_ex):
+        pick = jnp.concatenate([picked(expert, p).astype(F32) for p in range(parts)], axis=0).astype(BF16)
+        outgoing[expert * parts : (expert + 1) * parts] = (
+            dot(pick, tokens[...]).astype(BF16).reshape(parts, piece, width)
+        )
+    for p in range(parts):
+        block(rows_in, (0,), e, p)[...] = outgoing[e * parts + p]
+    wide = tokens[...].astype(F32)
+    own_squares = jnp.sum(wide * wide, axis=1, keepdims=True)
+    own_squares = jnp.sum(jnp.where(tok_rows == tok_lanes, own_squares, 0.0), axis=0, keepdims=True)
+    squares[t] = jnp.broadcast_to(own_squares, (8, tok))
+    with SCOPE("barrier"):
+        pl.semaphore_wait(barrier, n_dp + n_ex + n_t - 3)
+    for step in range(1, n_t):
+        copy(squares.at[t], squares.at[t], sq, rq, tensor=at(t, step, n_t)).start()
+
+    def normalize():
+        pending(squares.at[: n_t - 1], rq).wait()
+        total = squares[0, 0:1, :]
+        for s in range(1, n_t):
+            total = total + squares[s, 0:1, :]
+        scale = lax.rsqrt(total / width_all + 1e-06)
+        tile_rows = lax.broadcasted_iota(jnp.int32, (8, tok), 0)
+        for expert in range(n_ex):
+            tile = jnp.zeros((8, tok), F32)
+            for p in range(parts):
+                column = jnp.sum(jnp.where(picked(expert, p), scale, 0.0), axis=1, keepdims=True)
+                row = jnp.sum(jnp.where(diagonal, column, 0.0), axis=0, keepdims=True)
+                tile = jnp.where(tile_rows == p, row, tile)
+            scale_out[expert] = tile
+        scales_in[0, e] = scale_out[e]
+        for step in range(1, n_ex):
+            to = at(e, step, n_ex)
+            copy(scale_out.at[to], scales_in.at[0, e], sn, rn.at[0], expert=to).start()
+
+    def spread():
+        pending(scales_in.at[0, : n_ex - 1], rn.at[0]).wait()
+        for hop in range(1, n_dp):
+            copy(scales_in.at[0], scales_in.at[n_dp - hop], sm, rn.at[n_dp - hop], dp=at(d, hop, n_dp)).start()
 
     def send(q, p):
         for i in range(group):
             expert = q * group + i
-            out = dot(picked(expert, p).astype(BF16), tokens[...]).astype(BF16)
 
             @pl.when(expert != e)
             def _():
-                outgoing[expert * parts + p] = out
                 z_copy(expert, p).start()
-
-            @pl.when(expert == e)
-            def _():
-                block(rows_in, (0,), e, p)[...] = out
 
     def forward(q, p):
         for i in range(group):
@@ -232,37 +280,32 @@
         for hop in range(1, n_dp):
             x_copy(q * parts + p, hop).start()
 
-    diagonal = lax.broadcasted_iota(jnp.int32, (rows, 2 * sub), 0) == lax.broadcasted_iota(jnp.int32, (rows, 2 * sub), 1)
-    extra_rows = lax.broadcasted_iota(jnp.int32, (EXTRA, 2 * sub), 0)
-
     def project(h, u):
         @pl.when(h > 0)
         def _():
-            copy(rows_in.at[0, u], rows_in.at[h, u], sx, rx.at[h - 1, u], "dp", at(d, h, n_dp)).wait_recv()
+            copy(rows_in.at[0, u], rows_in.at[h, u], sx, rx.at[h - 1, u], dp=at(d, h, n_dp)).wait_recv()
 
         block_rows = rows_in[h, u]
-        wide = block_rows.astype(F32)
-        squares = jnp.sum(wide * wide, axis=1, keepdims=True)
-        squares = jnp.sum(jnp.where(diagonal, squares, 0.0), axis=0, keepdims=True)
-        high = squares.astype(BF16).astype(F32)
-        extra = jnp.where(extra_rows == 0, high, jnp.where(extra_rows == 1, squares - high, 0.0)).astype(BF16)
-        for to in range(n_t):
-            part[h, u, to, rows:, :] = extra
         for g in range(2):
             sums = dot(block_rows, w_in[g]).astype(BF16)
             for to in range(n_t):
-                part[h, u, to, :rows, g * sub : (g + 1) * sub] = sums[:, to * sub : (to + 1) * sub]
+                part[h, u, to, :, g * sub : (g + 1) * sub] = sums[:, to * sub : (to + 1) * sub]
         for step in range(1, n_t):
             part_copy(h, u, step).start()
 
-    def activate(h, u):
+    def activate(h, q, p):
+        u = q * parts + p
         pending(part_in.at[h, u, : n_t - 1], rp.at[h, u]).wait()
         total = part[h, u, t].astype(F32)
         for step in range(1, n_t):
             total = total + part_in[h, u, at(t, step, n_t)].astype(F32)
-        squares = jnp.sum(total[rows:], axis=0, keepdims=True)
-        squares = jnp.sum(jnp.where(diagonal, squares, 0.0), axis=1, keepdims=True)
-        total = total[:rows] * lax.rsqrt(squares / width_all + 1e-06)
+        scale = [
+            jnp.sum(
+                jnp.where(diagonal, scales_in[h, q * group + i, pl.ds(p, 1), :], 0.0), axis=1, keepdims=True
+            )
+            for i in range(group)
+        ]
+        total = total * jnp.concatenate(scale, axis=0)
         gate, up = total[:, :sub], total[:, sub:]
         hidden[h, u, t] = (gate / (1.0 + jnp.exp(-gate)) * up).astype(BF16)
         for step in range(1, n_t):
@@ -287,7 +330,7 @@
         total = keep[u]
         for h in range(1, n_dp):
             copy(
-                down.at[h - 1, u], down_in.at[h - 1, u], so, ro.at[h - 1, u], "dp", at(d, h, n_dp)
+                down.at[h - 1, u], down_in.at[h - 1, u], so, ro.at[h - 1, u], dp=at(d, h, n_dp)
             ).wait_recv()
             total = total + down_in[h - 1, u].astype(F32)
         home[u] = total.astype(BF16)
@@ -303,12 +346,20 @@
                 home_in[expert * parts + p] = home[u, i * piece : (i + 1) * piece]
 
     first_project = min(i for i, op in enumerate(plan) if op[0] == PROJECT)
+    first_activate = min(i for i, op in enumerate(plan) if op[0] == ACTIVATE)
+    first_far_activate = [min(i for i, op in enumerate(plan) if op[:2] == (ACTIVATE, h)) for h in range(1, n_dp)]
+    first_far = min(i for i, op in enumerate(plan) if op[0] in (FORWARD, ACTIVATE) and op[2] + (op[0] == ACTIVATE) > 0)
     first_expand = min(i for i, op in enumerate(plan) if op[0] == EXPAND)
 
     codes = [kind + 8 * (h + n_dp * (p + parts * o)) for kind, h, o, p in plan]
 
     @pl.loop(0, len(plan))
     def _(step):
+        @pl.when(step == first_far)
+        def _():
+            with SCOPE("normalize"):
+                normalize()
+
         code = lookup(codes, step)
         kind, rest = lax.rem(code, 8), code // 8
         h, rest = lax.rem(rest, n_dp), rest // n_dp
@@ -337,8 +388,17 @@
 
         @pl.when(kind == ACTIVATE)
         def _():
+            @pl.when(step == first_activate)
+            def _():
+                spread()
+
+            for hop in range(1, n_dp):
+                @pl.when(step == first_far_activate[hop - 1])
+                def _():
+                    pending(scales_in.at[hop], rn.at[hop]).wait()
+
             with SCOPE("activate"):
-                activate(h, u)
+                activate(h, q, p)
 
         @pl.when(kind == EXPAND)
         def _():
@@ -354,28 +414,39 @@
             with SCOPE("collect"):
                 collect(q, p)
 
+    load_scores.wait()
     weights = []
     for expert in range(n_ex):
         score = jnp.zeros((1, tok), F32)
         for k in range(top):
             score = score + jnp.where(ids[k : k + 1, :] == expert, scores[k : k + 1, :].astype(F32), 0.0)
-        weights += [picked(expert, p) * score for p in range(parts)]
+        weights += [jnp.where(picked(expert, p), score, 0.0) for p in range(parts)]
     combine = jnp.transpose(jnp.concatenate(weights, axis=0)).astype(BF16)
 
     others = (n_ex - 1) * parts
     with SCOPE("homes"):
         pending(home_in.at[:others], rr).wait()
 
+    stores = []
     with SCOPE("mix"):
-        mixed[...] = dot(combine, home_in[...].reshape(n_ex * cap, width)).astype(BF16)
+        for i, start in enumerate(range(0, width, width // 2)):
+            columns = slice(start, start + width // 2)
+            result[:, columns] = dot(combine, home_in[:, :, columns].reshape(n_ex * cap, width // 2)).astype(BF16)
+            stores.append(pltpu.make_async_copy(result.at[:, columns], mixed.at[:, columns], local_sem.at[i]))
+            stores[i].start()
 
     with SCOPE("drain"):
+        pending(squares.at[: n_t - 1], sq).wait()
+        pending(scales_in.at[0, : n_ex - 1], sn).wait()
+        pending(scales_in.at[1:], sm).wait()
         pending(outgoing.at[:others], sz).wait()
         pending(home_in.at[:others], sr).wait()
         pending(down, so).wait()
         pending(rows_in.at[1:], sx).wait()
         pending(part.at[:, :, : n_t - 1], sp).wait()
         pending(hidden.at[:, :, : n_t - 1], sh).wait()
+        for store in stores:
+            store.wait()
 
 
 SCOPE = jax.named_scope
@@ -391,29 +462,40 @@
     rows = group * piece
     plan = make_plan(n_dp, chunks, parts)
     dma = pltpu.SemaphoreType.DMA
-    vmem = pl.BlockSpec(memory_space=pltpu.VMEM)
+    top = ids.shape[0]
     hbm = pl.BlockSpec(memory_space=pl.ANY)
     return pl.pallas_call(
         functools.partial(kernel, sizes, plan),
         out_shape=jax.ShapeDtypeStruct((tok, width), BF16),
-        in_specs=[hbm, vmem, vmem, hbm, hbm],
-        out_specs=vmem,
+        in_specs=[hbm] * 5,
+        out_specs=hbm,
         scratch_shapes=[
             pltpu.VMEM((tok, width), BF16),
+            pltpu.VMEM((top, tok), jnp.int32),
+            pltpu.VMEM((top, tok), BF16),
             pltpu.VMEM((2, width, units), BF16),
             pltpu.VMEM((units, width), BF16),
             pltpu.VMEM((max(128, n_ex), tok), F32),
+            pltpu.VMEM((n_t, 8, tok), F32),
+            pltpu.VMEM((n_ex, 8, tok), F32),
+            pltpu.VMEM((n_dp, n_ex, 8, tok), F32),
             pltpu.VMEM((n_ex * parts, piece, width), BF16),
             pltpu.VMEM((n_dp, count, rows, width), BF16),
-            pltpu.VMEM((n_dp, count, n_t, rows + EXTRA, 2 * units // n_t), BF16),
-            pltpu.VMEM((n_dp, count, n_t, rows + EXTRA, 2 * units // n_t), BF16),
+            pltpu.VMEM((n_dp, count, n_t, rows, 2 * units // n_t), BF16),
+            pltpu.VMEM((n_dp, count, n_t, rows, 2 * units // n_t), BF16),
             pltpu.VMEM((n_dp, count, n_t, rows, units // n_t), BF16),
             pltpu.VMEM((count, rows, width), F32),
             pltpu.VMEM((n_dp - 1, count, rows, width), BF16),
             pltpu.VMEM((n_dp - 1, count, rows, width), BF16),
             pltpu.VMEM((count, rows, width), BF16),
             pltpu.VMEM((n_ex * parts, piece, width), BF16),
-            dma((3,)),
+            pltpu.VMEM((tok, width), BF16),
+            dma((5,)),
+            dma,
+            dma,
+            dma,
+            dma,
+            dma((n_dp,)),
             dma,
             dma((n_ex * parts,)),
             dma,
@@ -440,7 +522,7 @@
         tok = tokens.shape[0] // (n_dp * n_ex)
         slots = min(3 * tok * expert_ids.shape[1] // (2 * n_ex), tok)
         group = max(1, n_ex // n_t)
-        parts = 2 if group == 1 else 1
+        parts = 3 if group == 1 else 1
         cap = -(-slots // (16 * parts)) * 16 * parts
         return jax.shard_map(
             functools.partial(per_device, (n_dp, n_ex, n_t, cap, group, parts)),

time: 86.8 us -> 74.9 us (0.86)
  Pallas kernels: 84.8 us -> 72.9 us
    pallas_call x1, Pallas kernels: 84.8 us -> 72.9 us  [per_device(): pl.pallas_call(functools.partial(kernel, sizes, plan), out_shape=jax.Shap...]
where the time goes in v3:
time: 74.9 us; the launch traced here: 74.7 us
  Pallas kernels  72.9 us (97%)
  local copies, waits for them, and re-layouts  1.82 us (2%)
    pallas_call x1, Pallas kernels, per_device(): pl.pallas_call(functools.partial(kernel, sizes, plan), out_shape=jax.Shap...  72.9 us
    unnamed x1, local copies, waits for them, and re-layouts  1.82 us

profile of v3, /device:TPU:0, one launch (start us, length us, event | category | flops | bytes accessed | tf_op | source)
XLA Modules:
  0.0 74.7 jit_solution(14101458225056331449)
XLA Ops:
  0.0 72.9 %shard_map.55 = bf16[128,1792]{1,0:T(8,128)(2,1)} custom-call(bf16[128,1792]{1,0:T(8,128)(2,1)} %tokens_hbm.1, s32[2,128]{1,0:T(2,128)} %bitcast.2, bf16[2,128]{1,0:T(2,128)(2,1)} %bitcast.3, bf16[1,2,1792,512]{3,2,1,0:T(8,128)(2,1)} %w_in_hbm.1, bf16[1,512,1792]{2,1,0:T(8,128)(2,1)} %w_out_hbm.1), custom_call_target="tpu_custom_call" | custom-call | tf_op jit(solution)/shard_map/pallas_call | solution.py:467
  72.9 1.8 %copy.7 = bf16[128,1792]{1,0:T(8,128)(2,1)} copy(bf16[128,1792]{1,0:T(8,128)(2,1)} %shard_map.55) | data formatting | bytes 917504

commit v4 on v3

--- a/solution.py
+++ b/solution.py
@@ -10,18 +10,18 @@
 MESH = pl.DeviceIdType.MESH
 F32 = jnp.float32
 BF16 = jnp.bfloat16
-SEND, FORWARD, PROJECT, ACTIVATE, EXPAND, COLLECT = range(6)
-KINDS = "SFPAEC"
+SEND, FORWARD, PROJECT, ACTIVATE, EXPAND, COLLECT, NORMALIZE, SPREAD = range(8)
+KINDS = "SFPAECNG"
 TUNED = (
-    "S011", "F001", "P001", "S012", "F002", "P000", "P002", "S031", "F011", "S030", "S032", "P011",
-    "F012", "P102", "F031", "S020", "P012", "P031", "P101", "S022", "F000", "P112", "F030", "P111",
-    "P131", "A012", "F032", "A111", "A131", "F020", "A112", "S021", "P100", "P020", "S010", "F022",
-    "A031", "P132", "A011", "A002", "E112", "E111", "P120", "P032", "P122", "P022", "E012", "E131",
-    "C012", "A020", "A120", "A132", "A032", "F021", "E011", "A122", "C011", "E031", "P021", "A022",
-    "A001", "E020", "C031", "E122", "E032", "F010", "E120", "P121", "E022", "P130", "C022", "P010",
-    "A021", "E132", "A121", "P110", "A130", "P030", "C020", "E121", "A110", "A010", "E001", "A100",
-    "E130", "A030", "C032", "A101", "A000", "E021", "C021", "E110", "E010", "A102", "E030", "E101",
-    "E100", "C030", "E102", "C010", "E002", "E000", "C000", "C001", "C002",
+    "S032", "S012", "S010", "F000", "F002", "N000", "F032", "P032", "S021", "P002", "F001", "P000",
+    "P001", "F012", "P102", "G000", "P132", "F010", "P010", "P012", "S022", "A001", "P101", "A032",
+    "A132", "F021", "P021", "A002", "P100", "A012", "S031", "S030", "E132", "P112", "F022", "P121",
+    "P110", "A021", "A112", "F031", "S020", "A121", "F030", "P031", "P122", "A000", "S011", "P022",
+    "E121", "E032", "A010", "A102", "E112", "C032", "E012", "A122", "A110", "E021", "P131", "F020",
+    "C021", "A022", "E122", "P130", "P030", "C012", "A131", "F011", "E022", "A101", "P011", "P120",
+    "P020", "A100", "E110", "A130", "C022", "E131", "A120", "A030", "A031", "E010", "P111", "E130",
+    "C010", "A011", "E031", "E120", "C031", "E000", "A020", "E030", "A111", "E100", "C030", "E001",
+    "E020", "E111", "E102", "E002", "E011", "C020", "E101", "C011", "C000", "C001", "C002",
 )
 
 
@@ -56,6 +56,7 @@
     for o, p in own:
         plan += [(FORWARD, 0, o, p)]
     count = len(units)
+    plan += [(NORMALIZE, 0, 0, 0), (SPREAD, 0, 0, 0)]
     for s in range(count + 4):
         if parts <= s + 1 < count:
             plan.append((FORWARD, 0, *units[s + 1]))
@@ -98,6 +99,7 @@
     home,
     home_in,
     result,
+    combine,
     local_sem,
     sq,
     rq,
@@ -256,6 +258,16 @@
             to = at(e, step, n_ex)
             copy(scale_out.at[to], scales_in.at[0, e], sn, rn.at[0], expert=to).start()
 
+    def weigh():
+        load_scores.wait()
+        weights = []
+        for expert in range(n_ex):
+            score = jnp.zeros((1, tok), F32)
+            for k in range(top):
+                score = score + jnp.where(ids[k : k + 1, :] == expert, scores[k : k + 1, :].astype(F32), 0.0)
+            weights += [jnp.where(picked(expert, p), score, 0.0) for p in range(parts)]
+        combine[...] = jnp.transpose(jnp.concatenate(weights, axis=0)).astype(BF16)
+
     def spread():
         pending(scales_in.at[0, : n_ex - 1], rn.at[0]).wait()
         for hop in range(1, n_dp):
@@ -346,20 +358,13 @@
                 home_in[expert * parts + p] = home[u, i * piece : (i + 1) * piece]
 
     first_project = min(i for i, op in enumerate(plan) if op[0] == PROJECT)
-    first_activate = min(i for i, op in enumerate(plan) if op[0] == ACTIVATE)
-    first_far_activate = [min(i for i, op in enumerate(plan) if op[:2] == (ACTIVATE, h)) for h in range(1, n_dp)]
-    first_far = min(i for i, op in enumerate(plan) if op[0] in (FORWARD, ACTIVATE) and op[2] + (op[0] == ACTIVATE) > 0)
+    first_far = [min(i for i, op in enumerate(plan) if op[:2] == (ACTIVATE, h)) for h in range(1, n_dp)]
     first_expand = min(i for i, op in enumerate(plan) if op[0] == EXPAND)
 
     codes = [kind + 8 * (h + n_dp * (p + parts * o)) for kind, h, o, p in plan]
 
     @pl.loop(0, len(plan))
     def _(step):
-        @pl.when(step == first_far)
-        def _():
-            with SCOPE("normalize"):
-                normalize()
-
         code = lookup(codes, step)
         kind, rest = lax.rem(code, 8), code // 8
         h, rest = lax.rem(rest, n_dp), rest // n_dp
@@ -388,12 +393,8 @@
 
         @pl.when(kind == ACTIVATE)
         def _():
-            @pl.when(step == first_activate)
-            def _():
-                spread()
-
             for hop in range(1, n_dp):
-                @pl.when(step == first_far_activate[hop - 1])
+                @pl.when(step == first_far[hop - 1])
                 def _():
                     pending(scales_in.at[hop], rn.at[hop]).wait()
 
@@ -409,19 +410,23 @@
             with SCOPE("expand"):
                 expand(h, u)
 
+        @pl.when(kind == NORMALIZE)
+        def _():
+            with SCOPE("normalize"):
+                normalize()
+
+        @pl.when(kind == SPREAD)
+        def _():
+            with SCOPE("weigh"):
+                weigh()
+
+            with SCOPE("spread"):
+                spread()
+
         @pl.when(kind == COLLECT)
         def _():
             with SCOPE("collect"):
                 collect(q, p)
-
-    load_scores.wait()
-    weights = []
-    for expert in range(n_ex):
-        score = jnp.zeros((1, tok), F32)
-        for k in range(top):
-            score = score + jnp.where(ids[k : k + 1, :] == expert, scores[k : k + 1, :].astype(F32), 0.0)
-        weights += [jnp.where(picked(expert, p), score, 0.0) for p in range(parts)]
-    combine = jnp.transpose(jnp.concatenate(weights, axis=0)).astype(BF16)
 
     others = (n_ex - 1) * parts
     with SCOPE("homes"):
@@ -431,7 +436,7 @@
     with SCOPE("mix"):
         for i, start in enumerate(range(0, width, width // 2)):
             columns = slice(start, start + width // 2)
-            result[:, columns] = dot(combine, home_in[:, :, columns].reshape(n_ex * cap, width // 2)).astype(BF16)
+            result[:, columns] = dot(combine[...], home_in[:, :, columns].reshape(n_ex * cap, width // 2)).astype(BF16)
             stores.append(pltpu.make_async_copy(result.at[:, columns], mixed.at[:, columns], local_sem.at[i]))
             stores[i].start()
 
@@ -490,6 +495,7 @@
             pltpu.VMEM((count, rows, width), BF16),
             pltpu.VMEM((n_ex * parts, piece, width), BF16),
             pltpu.VMEM((tok, width), BF16),
+            pltpu.VMEM((tok, n_ex * cap), BF16),
             dma((5,)),
             dma,
             dma,

time: 74.9 us -> 72.8 us (0.972)
  Pallas kernels: 72.9 us -> 70.8 us
    pallas_call x1, Pallas kernels: 72.9 us -> 70.8 us  [per_device(): pl.pallas_call(functools.partial(kernel, sizes, plan), out_shape=jax.Shap...]
where the time goes in v4:
time: 72.8 us; the launch traced here: 72.7 us
  Pallas kernels  70.8 us (97%)
  local copies, waits for them, and re-layouts  1.82 us (2%)
    pallas_call x1, Pallas kernels, per_device(): pl.pallas_call(functools.partial(kernel, sizes, plan), out_shape=jax.Shap...  70.8 us
    unnamed x1, local copies, waits for them, and re-layouts  1.82 us

profile of v4, /device:TPU:0, one launch (start us, length us, event | category | flops | bytes accessed | tf_op | source)
XLA Modules:
  0.0 72.7 jit_solution(9259966240936454233)
XLA Ops:
  0.0 70.8 %shard_map.55 = bf16[128,1792]{1,0:T(8,128)(2,1)} custom-call(bf16[128,1792]{1,0:T(8,128)(2,1)} %tokens_hbm.1, s32[2,128]{1,0:T(2,128)} %bitcast.2, bf16[2,128]{1,0:T(2,128)(2,1)} %bitcast.3, bf16[1,2,1792,512]{3,2,1,0:T(8,128)(2,1)} %w_in_hbm.1, bf16[1,512,1792]{2,1,0:T(8,128)(2,1)} %w_out_hbm.1), custom_call_target="tpu_custom_call" | custom-call | tf_op jit(solution)/shard_map/pallas_call | solution.py:472
  70.9 1.8 %copy.7 = bf16[128,1792]{1,0:T(8,128)(2,1)} copy(bf16[128,1792]{1,0:T(8,128)(2,1)} %shard_map.55) | data formatting | bytes 917504
